TPU v7x, 512 devices: a whole 4x4x16 slice. The times are simulated.
512 devices in a mesh: gx: 32 (over z, x_lo), gy: 16 (over y, x_hi, core).
Axes of the slice: x: 4 (x_hi: 2, x_lo: 2; x = x_hi * 2 + x_lo), y: 4, z: 16, core: 2. Of those that a mesh axis runs over, the one named last changes fastest.
Arguments:
- field: float32 [256, 128, 192], P('gx', 'gy'), may hold values from -6 to 6
- target: float32 [256, 128, 192], P('gx', 'gy'), may hold values from -6 to 6
- embed_weight: float32 [192, 256], replicated, may hold values from -0.4375 to 0.4375
- norm_gain: float32 [256], replicated, may hold values from 0.5 to 1.5
- attend_weight: float32 [256, 768], replicated, may hold values from -0.375 to 0.375
- output_weight: float32 [256, 256], replicated, may hold values from -0.375 to 0.375
- second_gain: float32 [256], replicated, may hold values from 0.5 to 1.5
- expand_weight: float32 [256, 512], replicated, may hold values from -0.375 to 0.375
- reduce_weight: float32 [512, 256], replicated, may hold values from -0.25 to 0.25
- decode_weight: float32 [256, 192], replicated, may hold values from -0.375 to 0.375
Outputs:
- loss: float32 [], replicated
- field_gradient: float32 [256, 128, 192], P('gx', 'gy')
- embed_gradient: float32 [192, 256], replicated
- norm_gradient: float32 [256], replicated
- attend_gradient: float32 [256, 768], replicated
- output_gradient: float32 [256, 256], replicated
- second_gradient: float32 [256], replicated
- expand_gradient: float32 [256, 512], replicated
- reduce_gradient: float32 [512, 256], replicated
- decode_gradient: float32 [256, 192], replicated
All inputs are finite; a program needn't handle non-finite values.
Results may differ from a plain program's by a relative error of at most 0.0001.
Values sent between devices are 32-bit elements; how exact they have to be, the bound alone decides.
No kernel may reach another device: no remote copies, remote signals or barrier semaphores. Data moves between devices by JAX's collectives and lax.ppermute only.
A program may use at most 128 MiB of HBM per device.

v0:
```python
import jax
import jax.numpy as jnp
from jax import lax
from jax.sharding import PartitionSpec as P

PATCH = 4
HEADS = 8
STEPS = 2
EXACT = lax.Precision.HIGHEST
EPSILON = 1e-06
TIME_STEP = 0.1
VISCOSITY = 0.5


def with_halo(x, sides, width):
    for axis, dim in sides:
        count, length = (lax.axis_size(axis), x.shape[dim])
        up = [(i, (i + 1) % count) for i in range(count)]
        down = [(j, i) for i, j in up]
        last = lax.slice_in_dim(x, length - width, length, axis=dim)
        leading = lax.slice_in_dim(x, 0, width, axis=dim)
        before = lax.ppermute(last, axis, up)
        after = lax.ppermute(leading, axis, down)
        x = jnp.concatenate([before, x, after], axis=dim)
    return x


def matmul(left, right):
    return jnp.dot(left, right, precision=EXACT)


def rms_scale(values, gain):
    power = jnp.mean(values * values, axis=-1, keepdims=True)
    return values * lax.rsqrt(power + EPSILON) * gain


def closure(ext, params):
    (
        embed_weight,
        norm_gain,
        attend_weight,
        output_weight,
        second_gain,
        expand_weight,
        reduce_weight,
        decode_weight,
    ) = params
    wide, tall, depth = ext.shape
    levels = depth // 3
    across, along, upward = (wide // PATCH, tall // PATCH, levels // PATCH)
    patches = ext.reshape(across, PATCH, along, PATCH, 3, upward, PATCH).transpose(
        0, 2, 5, 4, 1, 3, 6
    )
    patches = patches.reshape(across, along, upward, 3 * PATCH * PATCH * PATCH)
    tokens = matmul(patches, embed_weight)
    width = tokens.shape[-1]
    head_size = width // HEADS
    mixed = matmul(rms_scale(tokens, norm_gain), attend_weight)
    inner_x, inner_y = (across - 2, along - 2)
    queries = mixed[1:-1, 1:-1, :, :width].reshape(inner_x, inner_y, upward, HEADS, head_size)
    keyset = mixed[:, :, :, width : 2 * width]
    valset = mixed[:, :, :, 2 * width :]
    offsets = [(shift_x, shift_y) for shift_x in range(3) for shift_y in range(3)]
    keyblock = jnp.concatenate(
        [keyset[sx : sx + inner_x, sy : sy + inner_y] for sx, sy in offsets], axis=2
    )
    valblock = jnp.concatenate(
        [valset[sx : sx + inner_x, sy : sy + inner_y] for sx, sy in offsets], axis=2
    )
    keyblock = keyblock.reshape(inner_x, inner_y, 9 * upward, HEADS, head_size)
    valblock = valblock.reshape(inner_x, inner_y, 9 * upward, HEADS, head_size)
    factor = head_size ** (-0.5)
    scores = jnp.einsum("xyzhe,xywhe->xyhzw", queries, keyblock, precision=EXACT) * factor
    weights = jnp.exp(scores)
    weights = weights / jnp.sum(weights, axis=-1, keepdims=True)
    attended = jnp.einsum("xyhzw,xywhe->xyzhe", weights, valblock, precision=EXACT)
    attended = attended.reshape(inner_x, inner_y, upward, width)
    middle = tokens[1:-1, 1:-1] + matmul(attended, output_weight)
    hidden = jax.nn.silu(matmul(rms_scale(middle, second_gain), expand_weight))
    middle = middle + matmul(hidden, reduce_weight)
    result = matmul(middle, decode_weight).reshape(inner_x, inner_y, upward, 3, PATCH, PATCH, PATCH)
    return result.transpose(0, 4, 1, 5, 3, 2, 6).reshape(inner_x * PATCH, inner_y * PATCH, depth)


def advance(ext, params):
    wide, tall, depth = ext.shape
    levels = depth // 3
    inner = ext[PATCH : wide - PATCH, PATCH : tall - PATCH]
    east = ext[PATCH + 1 : wide - PATCH + 1, PATCH : tall - PATCH]
    west = ext[PATCH - 1 : wide - PATCH - 1, PATCH : tall - PATCH]
    north = ext[PATCH : wide - PATCH, PATCH + 1 : tall - PATCH + 1]
    south = ext[PATCH : wide - PATCH, PATCH - 1 : tall - PATCH - 1]
    level = jnp.arange(depth, dtype=jnp.int32) % levels
    blank = jnp.zeros(inner.shape[:2] + (1,), jnp.float32)
    upper = jnp.where(level == levels - 1, 0.0, jnp.concatenate([inner[:, :, 1:], blank], axis=2))
    lower = jnp.where(level == 0, 0.0, jnp.concatenate([blank, inner[:, :, :-1]], axis=2))
    laplace = east + west + north + south + upper + lower - 6.0 * inner
    speed_x = jnp.concatenate([inner[:, :, 0:levels]] * 3, axis=2)
    speed_y = jnp.concatenate([inner[:, :, levels : 2 * levels]] * 3, axis=2)
    speed_z = jnp.concatenate([inner[:, :, 2 * levels :]] * 3, axis=2)
    carried = 0.5 * (
        speed_x * (east - west) + speed_y * (north - south) + speed_z * (upper - lower)
    )
    return inner + TIME_STEP * (VISCOSITY * laplace - carried + closure(ext, params))


def fold(spread, margin):
    for axis_dim in (0, 1):
        length = spread.shape[axis_dim] - 4 * margin
        middle = lax.slice_in_dim(spread, 2 * margin, 2 * margin + length, axis=axis_dim)
        lowside = lax.slice_in_dim(spread, 0, margin, axis=axis_dim)
        highside = lax.slice_in_dim(spread, length + 3 * margin, length + 4 * margin, axis=axis_dim)
        pad_low = [(0, 0), (0, 0), (0, 0)]
        pad_high = [(0, 0), (0, 0), (0, 0)]
        pad_low[axis_dim] = (0, length - margin)
        pad_high[axis_dim] = (length - margin, 0)
        spread = middle + jnp.pad(lowside, pad_low) + jnp.pad(highside, pad_high)
    return spread


def shards(
    field,
    target,
    embed_weight,
    norm_gain,
    attend_weight,
    output_weight,
    second_gain,
    expand_weight,
    reduce_weight,
    decode_weight,
):
    params = (
        embed_weight,
        norm_gain,
        attend_weight,
        output_weight,
        second_gain,
        expand_weight,
        reduce_weight,
        decode_weight,
    )
    energy = lax.psum(jnp.sum(target * target), ("gx", "gy"))
    current = field
    pullbacks = []
    for step in range(STEPS):
        extended = with_halo(current, (("gx", 0), ("gy", 1)), PATCH)
        current, pullback = jax.vjp(advance, extended, params)
        pullbacks.append(pullback)
    residue = current - target
    cotangent = 2.0 * residue
    gradients = None
    for pullback in reversed(pullbacks):
        back_ext, back_params = pullback(cotangent)
        gradients = (
            back_params if gradients is None else jax.tree.map(jnp.add, gradients, back_params)
        )
        spread = with_halo(back_ext, (("gx", 0), ("gy", 1)), PATCH)
        cotangent = fold(spread, PATCH)
    local_misfit = jnp.sum(residue * residue)
    misfit = lax.psum(local_misfit, ("gx", "gy"))
    summed = lax.psum(tuple(gradients), ("gx", "gy"))
    entries = (
        field.shape[0] * lax.axis_size("gx") * field.shape[1] * lax.axis_size("gy") * field.shape[2]
    )
    scale = jnp.float32(entries) / energy
    loss = misfit / energy
    return (loss, scale * cotangent) + tuple((scale * piece for piece in summed))


def solution(mesh):
    in_specs = (P("gx", "gy", None), P("gx", "gy", None), P(), P(), P(), P(), P(), P(), P(), P())
    out_specs = (P(), P("gx", "gy", None), P(), P(), P(), P(), P(), P(), P(), P())
    return jax.shard_map(shards, mesh=mesh, in_specs=in_specs, out_specs=out_specs, check_vma=False)
```

profile of v0, /device:TPU:1, one launch (start us, length us, event | category | flops | bytes accessed | tf_op | source)
XLA Modules:
  0.0 810.8 jit_solution(4378260794345569212)
XLA Ops:
  8.1 12.9 %collective-permute-start = (f32[4,8,192]{2,1,0:T(8,128)S(1)}, f32[4,8,192]{2,1,0:T(8,128)S(1)}, u32[]{:S(2)}, u32[]{:S(2)}) collective-permute-start(f32[4,8,192]{2,1,0:T(8,128)S(1)} %get-tuple-element.154), channel_id=1, source_target_pairs={{16,0},{32,16},{48,32},{64,48},{80,64},{96,80},{112,96},{128,112},... | collective-permute-start | bytes 73736 | tf_op jit(solution)/shard_map/ppermute | solution.py:23
  20.9 1.9 collective-permute-start.1
  29.2 6.3 collective-permute-start.3
  35.5 1.9 collective-permute-start.2
  38.2 4.5 collective-permute-done.2
  43.3 5.0 reshape.216
  48.4 6.5 copy.78
  54.9 2.7 multiply_reduce_fusion.7
  67.5 2.2 copy.85
  72.3 1.9 collective-permute-start.5
  74.2 5.5 collective-permute-start.4
  80.7 3.0 collective-permute-start.7
  83.7 1.9 collective-permute-start.6
  86.4 4.5 collective-permute-done.6
  90.9 5.0 reshape.224
  96.0 7.0 copy.86
  103.0 3.9 multiply_reduce_fusion.6
  111.8 1.9 fusion.184
  115.0 2.4 copy.88
  117.4 2.3 convolution_bitcast_fusion.10
  124.0 2.2 copy.93
  127.4 1.9 negate_add_fusion.3
  129.3 2.4 negate_add_fusion.2
  133.4 1.9 copy.94
  135.3 1.9 fusion.73
  138.8 2.1 multiply_reduce_fusion.9
  141.7 2.1 multiply_reduce_fusion.1
  146.6 2.2 fusion.36
  154.1 3.2 fusion.169
  158.4 1.8 copy.185
  160.3 1.9 copy.184
  162.2 1.9 copy.183
  171.2 3.0 fusion.170
  176.0 1.9 copy.194
  177.9 1.9 copy.193
  179.8 1.8 copy.192
  181.7 1.9 copy.191
  191.8 6.1 copy.118
  198.1 5.1 reshape.239
  203.7 1.9 collective-permute-start.8
  205.6 5.6 collective-permute-start.9
  212.6 3.2 collective-permute-start.10
  215.8 4.0 collective-permute-start.11
  220.4 3.1 collective-permute-done.11
  229.3 2.2 convolution_bitcast_fusion.12
  246.0 3.0 fusion.167
  249.1 1.8 copy.196
  250.9 1.9 copy.203
  252.8 1.9 copy.202
  262.6 3.3 fusion.168
  265.8 1.9 copy.205
  267.7 1.9 copy.212
  269.6 1.8 copy.211
  273.3 1.9 copy.209
  289.5 2.2 fusion.6
  293.5 6.3 copy.143
  299.8 5.0 reshape.247
  306.0 1.9 collective-permute-start.12
  307.9 5.5 collective-permute-start.13
  313.4 107.6 %all-reduce.72 = (f32[]{:T(128)}, f32[]{:T(128)}, f32[256]{0:T(256)S(1)}, f32[256]{0:T(256)S(1)}) all-reduce(f32[]{:T(128)} %get-tuple-element.141, f32[]{:T(128)} %multiply_reduce_fusion.12, f32[256]{0:T(256)S(1)} %add.385, f32[256]{0:T(256)S(1)} %add.388), channel_id=1, replica_groups=mesh['gx'=32,'gy'=16] {'gx','gy'}, use_global_device_ids=true, to_apply=%region_7.8 | all-reduce | flops 514 | bytes 4112 | tf_op jit(solution)/shard_map/psum | solution.py:161
  422.3 3.5 collective-permute-start.14
  425.9 1.9 collective-permute-start.15
  429.7 3.6 collective-permute-done.15
  434.2 360.8 %all-reduce.76.cloned.1.call-done = (f32[192,256]{1,0:T(8,128)}, f32[256,768]{1,0:T(8,128)}, f32[256,256]{1,0:T(8,128)}, f32[256,512]{1,0:T(8,128)}, f32[512,256]{1,0:T(8,128)}, /*index=5*/f32[256,192]{0,1:T(8,128)}) async-done(((f32[192,256]{1,0:T(8,128)}, f32[256,768]{1,0:T(8,128)}, f32[256,256]{1,0:T(8,128)}, f32[256,512]{1,0:T(8,128)}, f32[512,256]{1,0:T(8,128)}, /*index=5*/f32[256,192]{0,1:T(8,128)}), ...) | async-done | bytes 2490384 | tf_op jit(solution)/shard_map/psum | solution.py:162
  (592 shorter events, 122.3 us)
Async XLA Ops:
  7.2 51.0 %copy-start = (f32[256,768]{1,0:T(8,128)S(1)}, f32[256,768]{1,0:T(8,128)}, u32[]{:S(2)}) copy-start(f32[256,768]{1,0:T(8,128)} %param.14) | copy-start | bytes 2359300
  7.2 787.8 %all-reduce.76.cloned.1.call-start = ((), (), s32[]{:S(2)}) async-start(), calls=%async_computation | async-start | bytes 4980736 | tf_op jit(solution)/shard_map/psum | solution.py:162
  8.1 20.5 %collective-permute-start = (f32[4,8,192]{2,1,0:T(8,128)S(1)}, f32[4,8,192]{2,1,0:T(8,128)S(1)}, u32[]{:S(2)}, u32[]{:S(2)}) collective-permute-start(f32[4,8,192]{2,1,0:T(8,128)S(1)} %get-tuple-element.154), channel_id=1, source_target_pairs={{16,0},{32,16},{48,32},{64,48},{80,64},{96,80},{112,96},{128,112},... | collective-permute-start | bytes 73736 | tf_op jit(solution)/shard_map/ppermute | solution.py:23
  20.9 6.8 collective-permute-start.1
  28.6 14.0 %copy-start.36 = (f32[16,8,192]{2,1,0:T(8,128)}, f32[16,8,192]{2,1,0:T(8,128)S(1)}, u32[]{:S(2)}) copy-start(f32[16,8,192]{2,1,0:T(8,128)S(1)} %constant_dynamic-update-slice_fusion) | copy-start | bytes 294916
  29.2 9.0 %collective-permute-start.3 = (f32[16,4,192]{2,1,0:T(4,128)S(1)}, f32[16,4,192]{2,1,0:T(4,128)S(1)}, u32[]{:S(2)}, u32[]{:S(2)}) collective-permute-start(f32[16,4,192]{2,1,0:T(4,128)S(1)} %get-tuple-element.122), channel_id=1, source_target_pairs={{0,1},{1,2},{2,3},{3,4},{4,5},{5,6},{6,7},{7,8},{8,9},{9,10},{10,1... | collective-permute-start | bytes 147464 | tf_op jit(solution)/shard_map/ppermute | solution.py:22
  35.5 7.1 collective-permute-start.2
  37.5 33.5 %copy-start.191 = (pred[192]{0:T(512)(128)(4,1)}, pred[192]{0:T(512)(128)(4,1)S(1)}, u32[]{:S(2)}) copy-start(pred[192]{0:T(512)(128)(4,1)S(1)} %get-tuple-element.177) | copy-start | bytes 580
  37.5 33.5 %copy-start.196 = (pred[192]{0:T(512)(128)(4,1)}, pred[192]{0:T(512)(128)(4,1)S(1)}, u32[]{:S(2)}) copy-start(pred[192]{0:T(512)(128)(4,1)S(1)} %get-tuple-element.176) | copy-start | bytes 580
  48.4 6.6 copy-start.33
  72.3 8.1 %collective-permute-start.5 = (f32[4,8,192]{2,1,0:T(8,128)S(1)}, f32[4,8,192]{2,1,0:T(8,128)S(1)}, u32[]{:S(2)}, u32[]{:S(2)}) collective-permute-start(f32[4,8,192]{2,1,0:T(8,128)S(1)} %get-tuple-element.147), channel_id=1, source_target_pairs={{0,16},{16,32},{32,48},{48,64},{64,80},{80,96},{96,112},{112,128},... | collective-permute-start | bytes 73736 | tf_op jit(solution)/shard_map/ppermute | solution.py:22
  74.2 6.5 collective-permute-start.4
  80.4 15.5 %copy-start.111 = (f32[4,8,192]{2,1,0:T(8,128)}, f32[4,8,192]{2,1,0:T(8,128)S(1)}, u32[]{:S(2)}) copy-start(f32[4,8,192]{2,1,0:T(8,128)S(1)} %collective-permute-done.5) | copy-start | bytes 73732
  80.7 15.3 %copy-start.113 = (f32[4,8,192]{2,1,0:T(8,128)}, f32[4,8,192]{2,1,0:T(8,128)S(1)}, u32[]{:S(2)}) copy-start(f32[4,8,192]{2,1,0:T(8,128)S(1)} %collective-permute-done.4) | copy-start | bytes 73732
  80.7 5.6 collective-permute-start.7
  83.7 7.1 collective-permute-start.6
  86.4 9.6 %copy-start.102 = (f32[16,4,192]{2,1,0:T(4,128)}, f32[16,4,192]{2,1,0:T(4,128)S(1)}, u32[]{:S(2)}) copy-start(f32[16,4,192]{2,1,0:T(4,128)S(1)} %collective-permute-done.7) | copy-start | bytes 147460
  113.8 6.0 copy-start.16
  135.3 5.6 copy-start.190
  135.3 5.7 copy-start.43
  135.3 5.7 copy-start.176
  135.3 5.7 copy-start.180
  135.3 5.8 copy-start.21
  135.3 6.3 copy-start.17
  160.3 9.3 %copy-start.46 = (f32[2,2,16,256]{2,3,1,0:T(8,128)S(1)}, f32[2,2,16,256]{2,3,1,0:T(8,128)}, u32[]{:S(2)}) copy-start(f32[2,2,16,256]{2,3,1,0:T(8,128)} %get-tuple-element.57) | copy-start | bytes 196612
  162.2 8.2 %copy-start.45 = (f32[2,2,16,256]{2,3,1,0:T(8,128)S(1)}, f32[2,2,16,256]{2,3,1,0:T(8,128)}, u32[]{:S(2)}) copy-start(f32[2,2,16,256]{2,3,1,0:T(8,128)} %get-tuple-element.58) | copy-start | bytes 196612
  176.0 9.4 %copy-start.49 = (f32[2,2,16,256]{2,3,1,0:T(8,128)S(1)}, f32[2,2,16,256]{2,3,1,0:T(8,128)}, u32[]{:S(2)}) copy-start(f32[2,2,16,256]{2,3,1,0:T(8,128)} %get-tuple-element.65) | copy-start | bytes 196612
  177.9 8.3 %copy-start.47 = (f32[2,2,16,256]{2,3,1,0:T(8,128)S(1)}, f32[2,2,16,256]{2,3,1,0:T(8,128)}, u32[]{:S(2)}) copy-start(f32[2,2,16,256]{2,3,1,0:T(8,128)} %get-tuple-element.66) | copy-start | bytes 196612
  190.3 7.7 copy-start.163
  198.1 5.5 copy-start.135
  203.2 8.1 copy-start.132
  203.2 16.6 %copy-start.155 = (f32[2,2,8,16]{3,2,1,0:T(8,128)S(1)}, f32[2,2,8,16]{3,2,1,0:T(8,128)}, u32[]{:S(2)}) copy-start(f32[2,2,8,16]{3,2,1,0:T(8,128)} %copy-done.154) | copy-start | bytes 6148
  203.5 20.1 %copy-start.194 = (pred[8]{0:T(512)(128)(4,1)S(1)}, pred[8]{0:T(512)(128)(4,1)}, u32[]{:S(2)}) copy-start(pred[8]{0:T(512)(128)(4,1)} %constant.73.clone.1) | copy-start | bytes 28
  203.7 20.0 %copy-start.108 = (f32[8,8,64]{2,1,0:T(8,128)S(1)}, f32[8,8,64]{2,1,0:T(8,128)}, u32[]{:S(2)}) copy-start(f32[8,8,64]{2,1,0:T(8,128)} %get-tuple-element.152) | copy-start | bytes 49156
  203.7 8.3 %collective-permute-start.8 = (f32[4,16,192]{2,1,0:T(8,128)S(1)}, f32[4,16,192]{2,1,0:T(8,128)S(1)}, u32[]{:S(2)}, u32[]{:S(2)}) collective-permute-start(f32[4,16,192]{2,1,0:T(8,128)S(1)} %get-tuple-element.112), channel_id=1, source_target_pairs={{0,16},{16,32},{32,48},{48,64},{64,80},{80,96},{96,112},{112,128},... | collective-permute-start | bytes 147464 | tf_op jit(solution)/shard_map/ppermute | solution.py:22
  205.6 6.9 collective-permute-start.9
  211.9 12.5 %copy-start.37 = (f32[16,8,192]{2,1,0:T(8,128)S(1)}, f32[16,8,192]{2,1,0:T(8,128)}, u32[]{:S(2)}) copy-start(f32[16,8,192]{2,1,0:T(8,128)} %copy-done.36) | copy-start | bytes 294916
  211.9 12.5 %copy-start.90 = (f32[8,8,191]{2,1,0:T(8,128)S(1)}, f32[8,8,191]{2,1,0:T(8,128)}, u32[]{:S(2)}) copy-start(f32[8,8,191]{2,1,0:T(8,128)} %get-tuple-element.149) | copy-start | bytes 146692
  211.9 12.5 %copy-start.91 = (f32[8,8,191]{2,1,0:T(8,128)S(1)}, f32[8,8,191]{2,1,0:T(8,128)}, u32[]{:S(2)}) copy-start(f32[8,8,191]{2,1,0:T(8,128)} %get-tuple-element.150) | copy-start | bytes 146692
  211.9 12.5 %copy-start.95 = (f32[16,4,192]{2,1,0:T(4,128)S(1)}, f32[16,4,192]{2,1,0:T(4,128)}, u32[]{:S(2)}) copy-start(f32[16,4,192]{2,1,0:T(4,128)} %copy-done.94) | copy-start | bytes 147460
  211.9 12.5 %copy-start.97 = (f32[16,4,192]{2,1,0:T(4,128)S(1)}, f32[16,4,192]{2,1,0:T(4,128)}, u32[]{:S(2)}) copy-start(f32[16,4,192]{2,1,0:T(4,128)} %copy-done.96) | copy-start | bytes 147460
  211.9 12.5 %copy-start.124 = (f32[4,8,192]{2,1,0:T(8,128)S(1)}, f32[4,8,192]{2,1,0:T(8,128)}, u32[]{:S(2)}) copy-start(f32[4,8,192]{2,1,0:T(8,128)} %copy-done.123) | copy-start | bytes 73732
  212.0 12.5 %copy-start.126 = (f32[4,8,192]{2,1,0:T(8,128)S(1)}, f32[4,8,192]{2,1,0:T(8,128)}, u32[]{:S(2)}) copy-start(f32[4,8,192]{2,1,0:T(8,128)} %copy-done.125) | copy-start | bytes 73732
  212.0 12.5 %copy-start.128 = (f32[8,8,64]{2,1,0:T(8,128)S(1)}, f32[8,8,64]{2,1,0:T(8,128)}, u32[]{:S(2)}) copy-start(f32[8,8,64]{2,1,0:T(8,128)} %get-tuple-element.153) | copy-start | bytes 49156
  212.0 12.5 %copy-start.197 = (pred[192]{0:T(512)(128)(4,1)S(1)}, pred[192]{0:T(512)(128)(4,1)}, u32[]{:S(2)}) copy-start(pred[192]{0:T(512)(128)(4,1)} %copy-done.196) | copy-start | bytes 580
  212.6 7.8 collective-permute-start.10
  215.8 7.7 collective-permute-start.11
  227.4 5.9 copy-start.188
  227.5 6.0 copy-start.22
  231.5 5.8 copy-start.14
  250.9 9.3 %copy-start.50 = (f32[2,2,16,256]{2,3,1,0:T(8,128)S(1)}, f32[2,2,16,256]{2,3,1,0:T(8,128)}, u32[]{:S(2)}) copy-start(f32[2,2,16,256]{2,3,1,0:T(8,128)} %get-tuple-element.38) | copy-start | bytes 196612
  252.8 8.2 %copy-start.48 = (f32[2,2,16,256]{2,3,1,0:T(8,128)S(1)}, f32[2,2,16,256]{2,3,1,0:T(8,128)}, u32[]{:S(2)}) copy-start(f32[2,2,16,256]{2,3,1,0:T(8,128)} %get-tuple-element.39) | copy-start | bytes 196612
  265.8 9.4 %copy-start.52 = (f32[2,2,16,256]{2,3,1,0:T(8,128)S(1)}, f32[2,2,16,256]{2,3,1,0:T(8,128)}, u32[]{:S(2)}) copy-start(f32[2,2,16,256]{2,3,1,0:T(8,128)} %get-tuple-element.46) | copy-start | bytes 196612
  267.7 8.3 %copy-start.51 = (f32[2,2,16,256]{2,3,1,0:T(8,128)S(1)}, f32[2,2,16,256]{2,3,1,0:T(8,128)}, u32[]{:S(2)}) copy-start(f32[2,2,16,256]{2,3,1,0:T(8,128)} %get-tuple-element.47) | copy-start | bytes 196612
  305.2 8.2 %copy-start.198 = (f32[256]{0:T(256)S(1)}, f32[256]{0:T(256)}, u32[]{:S(2)}) copy-start(f32[256]{0:T(256)} %get-tuple-element.16) | copy-start | bytes 3076
  305.2 8.2 %copy-start.200 = (f32[256]{0:T(256)S(1)}, f32[256]{0:T(256)}, u32[]{:S(2)}) copy-start(f32[256]{0:T(256)} %get-tuple-element.14) | copy-start | bytes 3076
  305.2 8.2 %copy-start.199 = (f32[256]{0:T(256)S(1)}, f32[256]{0:T(256)}, u32[]{:S(2)}) copy-start(f32[256]{0:T(256)} %get-tuple-element.12) | copy-start | bytes 3076
  305.2 8.2 %copy-start.201 = (f32[256]{0:T(256)S(1)}, f32[256]{0:T(256)}, u32[]{:S(2)}) copy-start(f32[256]{0:T(256)} %get-tuple-element.10) | copy-start | bytes 3076
  305.2 128.2 %copy-start.195 = (pred[8]{0:T(512)(128)(4,1)S(1)}, pred[8]{0:T(512)(128)(4,1)}, u32[]{:S(2)}) copy-start(pred[8]{0:T(512)(128)(4,1)} %constant.73.clone.1) | copy-start | bytes 28
  306.0 116.3 %collective-permute-start.12 = (f32[4,16,192]{2,1,0:T(8,128)S(1)}, f32[4,16,192]{2,1,0:T(8,128)S(1)}, u32[]{:S(2)}, u32[]{:S(2)}) collective-permute-start(f32[4,16,192]{2,1,0:T(8,128)S(1)} %get-tuple-element.110), channel_id=1, source_target_pairs={{0,16},{16,32},{32,48},{48,64},{64,80},{80,96},{96,112},{112,128},... | collective-permute-start | bytes 147464 | tf_op jit(solution)/shard_map/ppermute | solution.py:22
  307.9 114.4 %collective-permute-start.13 = (f32[4,16,192]{2,1,0:T(8,128)S(1)}, f32[4,16,192]{2,1,0:T(8,128)S(1)}, u32[]{:S(2)}, u32[]{:S(2)}) collective-permute-start(f32[4,16,192]{2,1,0:T(8,128)S(1)} %get-tuple-element.111), channel_id=1, source_target_pairs={{16,0},{32,16},{48,32},{64,48},{80,64},{96,80},{112,96},{128,112},... | collective-permute-start | bytes 147464 | tf_op jit(solution)/shard_map/ppermute | solution.py:23
  422.3 7.4 collective-permute-start.14
  425.9 7.4 collective-permute-start.15
  795.0 5.9 copy-start.115
  (157 other events, 467.8 us)
Sparse Core Ops, SparseCore 0:
  305.3 489.6 all-reduce.75
where the time goes:
time: 823 us; the launch traced here: 811 us
  waiting for transfers between devices  379 us (46%)
  local copies, waits for them, and re-layouts  147 us (18%)
  blocking collectives  108 us (13%)
  matrix products  67.6 us (8%)
  starting transfers between devices  63 us (8%)
  other arithmetic  26.2 us (3%)
  between operations  20.3 us (2%)
    psum x1, waiting for transfers between devices, shards(): summed = lax.psum(tuple(gradients), ('gx', 'gy'))  361 us
    psum x1, blocking collectives, shards(): misfit = lax.psum(local_misfit, ('gx', 'gy'))  108 us
    unnamed x462, local copies, waits for them, and re-layouts  58.7 us
    dot_general x36, matrix products, matmul(): return jnp.dot(left, right, precision=EXACT)  49.2 us
    ppermute x8, starting transfers between devices, with_halo(): after = lax.ppermute(leading, axis, down)  39.2 us
    transpose x4, local copies, waits for them, and re-layouts, closure(): ext.reshape(across, PATCH, along, PATCH, 3, upward, PATCH)  25.9 us
    ppermute x8, starting transfers between devices, with_halo(): before = lax.ppermute(last, axis, up)  23.7 us
    reshape x4, local copies, waits for them, and re-layouts, closure(): ext.reshape(across, PATCH, along, PATCH, 3, upward, PATCH)  20.2 us
  transfers between devices with their start and end apart: 17, of which 8 were waited for; matrix products, arithmetic and copies ran while one was open for 1% of the time, Pallas kernels for 0%

commit v1 on v0

--- a/solution.py
+++ b/solution.py
@@ -159,7 +159,7 @@
         cotangent = fold(spread, PATCH)
     local_misfit = jnp.sum(residue * residue)
     misfit = lax.psum(local_misfit, ("gx", "gy"))
-    summed = lax.psum(tuple(gradients), ("gx", "gy"))
+    summed = lax.psum(lax.psum(tuple(gradients), "gx"), "gy")
     entries = (
         field.shape[0] * lax.axis_size("gx") * field.shape[1] * lax.axis_size("gy") * field.shape[2]
     )

time: 823 us -> 759 us (0.922)
  waiting for transfers between devices: 379 us -> 196 us
  blocking collectives: 108 us -> 222 us
    psum x1 -> x2, waiting for transfers between devices: 361 us -> 183 us  [shards(): summed = lax.psum(lax.psum(tuple(gradients), 'gx'), 'gy')]
    psum x0 -> x2, blocking collectives: none -> 119 us  [shards(): summed = lax.psum(lax.psum(tuple(gradients), 'gx'), 'gy')]
    ppermute x8, waiting for transfers between devices: 16.4 us -> 2.41 us  [with_halo(): after = lax.ppermute(leading, axis, down)]
    ppermute x8, waiting for transfers between devices: 1.71 us -> 10.7 us  [with_halo(): before = lax.ppermute(last, axis, up)]
  transfers between devices with their start and end apart: 17 -> 18, of which waited for: 8 -> 8; matrix products, arithmetic and copies ran while one was open for 1% -> 3% of each run, Pallas kernels for 0% -> 0%
where the time goes in v1:
time: 759 us; the launch traced here: 746 us
  blocking collectives  222 us (29%)
  waiting for transfers between devices  196 us (26%)
  local copies, waits for them, and re-layouts  147 us (19%)
  starting transfers between devices  68.2 us (9%)
  matrix products  65.8 us (9%)
  other arithmetic  27 us (4%)
  between operations  20.4 us (3%)
    psum x2, waiting for transfers between devices, shards(): summed = lax.psum(lax.psum(tuple(gradients), 'gx'), 'gy')  183 us
    psum x2, blocking collectives, shards(): summed = lax.psum(lax.psum(tuple(gradients), 'gx'), 'gy')  119 us
    psum x1, blocking collectives, shards(): misfit = lax.psum(local_misfit, ('gx', 'gy'))  104 us
    unnamed x462, local copies, waits for them, and re-layouts  60.1 us
    dot_general x36, matrix products, matmul(): return jnp.dot(left, right, precision=EXACT)  48.3 us
    ppermute x8, starting transfers between devices, with_halo(): after = lax.ppermute(leading, axis, down)  43 us
    transpose x4, local copies, waits for them, and re-layouts, closure(): ext.reshape(across, PATCH, along, PATCH, 3, upward, PATCH)  26 us
    ppermute x8, starting transfers between devices, with_halo(): before = lax.ppermute(last, axis, up)  25.2 us
  transfers between devices with their start and end apart: 18, of which 8 were waited for; matrix products, arithmetic and copies ran while one was open for 3% of the time, Pallas kernels for 0%

profile of v1, /device:TPU:1, one launch (start us, length us, event | category | flops | bytes accessed | tf_op | source)
XLA Modules:
  0.0 746.4 jit_solution(10070879635020597356)
XLA Ops:
  8.1 3.9 collective-permute-start.1
  12.0 10.9 %collective-permute-start = (f32[4,8,192]{2,1,0:T(8,128)S(1)}, f32[4,8,192]{2,1,0:T(8,128)S(1)}, u32[]{:S(2)}, u32[]{:S(2)}) collective-permute-start(f32[4,8,192]{2,1,0:T(8,128)S(1)} %get-tuple-element.162), channel_id=1, source_target_pairs={{16,0},{32,16},{48,32},{64,48},{80,64},{96,80},{112,96},{128,112},... | collective-permute-start | bytes 73736 | tf_op jit(solution)/shard_map/ppermute | solution.py:23
  27.5 2.9 collective-permute-start.2
  30.4 4.3 collective-permute-start.3
  35.3 2.0 collective-permute-done.3
  38.0 5.1 reshape.216
  43.1 6.5 copy.78
  49.7 2.7 multiply_reduce_fusion.7
  58.3 2.4 convolution_bitcast_fusion.11
  64.4 2.2 copy.85
  69.2 2.8 collective-permute-start.4
  72.0 2.5 collective-permute-start.5
  75.2 3.5 collective-permute-done.5
  78.8 9.9 %collective-permute-start.6 = (f32[16,4,192]{2,1,0:T(4,128)S(1)}, f32[16,4,192]{2,1,0:T(4,128)S(1)}, u32[]{:S(2)}, u32[]{:S(2)}) collective-permute-start(f32[16,4,192]{2,1,0:T(4,128)S(1)} %get-tuple-element.129), channel_id=1, source_target_pairs={{1,0},{2,1},{3,2},{4,3},{5,4},{6,5},{7,6},{8,7},{9,8},{10,9},{11,1... | collective-permute-start | bytes 147464 | tf_op jit(solution)/shard_map/ppermute | solution.py:23
  88.7 1.9 collective-permute-start.7
  92.0 5.1 reshape.224
  97.1 7.0 copy.86
  104.1 3.9 multiply_reduce_fusion.6
  110.7 2.4 copy.88
  122.4 2.2 copy.93
  125.8 1.9 negate_add_fusion.3
  127.7 2.4 negate_add_fusion.2
  133.4 1.9 copy.94
  135.3 1.9 fusion.73
  138.8 2.0 multiply_reduce_fusion.9
  141.5 2.3 multiply_reduce_fusion.1
  146.3 2.2 fusion.36
  153.1 3.2 fusion.170
  159.9 1.9 copy.193
  161.8 1.9 copy.192
  170.8 2.8 fusion.169
  173.7 1.9 copy.186
  187.9 2.2 multiply_reduce_fusion.3
  191.6 6.3 copy.118
  198.0 5.1 reshape.239
  203.6 1.9 collective-permute-start.9
  205.6 3.5 collective-permute-start.8
  209.1 3.7 collective-permute-done.8
  212.9 9.2 %collective-permute-start.11 = (f32[24,4,192]{2,1,0:T(4,128)S(1)}, f32[24,4,192]{2,1,0:T(4,128)S(1)}, u32[]{:S(2)}, u32[]{:S(2)}) collective-permute-start(f32[24,4,192]{2,1,0:T(4,128)S(1)} %get-tuple-element.117), channel_id=1, source_target_pairs={{1,0},{2,1},{3,2},{4,3},{5,4},{6,5},{7,6},{8,7},{9,8},{10,9},{11,1... | collective-permute-start | bytes 221192 | tf_op jit(solution)/shard_map/ppermute | solution.py:23
  222.1 2.1 collective-permute-start.10
  228.4 2.0 copy.119
  230.4 1.9 fusion.71
  233.9 2.0 multiply_reduce_fusion.8
  237.1 2.0 multiply_reduce_fusion
  243.7 3.0 fusion.168
  248.6 1.9 copy.212
  250.5 1.9 copy.211
  260.2 2.7 fusion.167
  262.9 1.9 copy.204
  275.7 2.2 multiply_reduce_fusion.2
  283.5 2.2 fusion.6
  293.6 103.6 %all-reduce.72 = (f32[]{:T(128)}, f32[]{:T(128)}) all-reduce(f32[]{:T(128)} %get-tuple-element.149, f32[]{:T(128)} %multiply_reduce_fusion.12), channel_id=1, replica_groups=mesh['gx'=32,'gy'=16] {'gx','gy'}, use_global_device_ids=true, to_apply=%region_7.8 | all-reduce | flops 2 | bytes 16 | tf_op jit(solution)/shard_map/psum | solution.py:161
  400.8 6.3 copy.143
  407.0 5.0 reshape.247
  412.2 132.2 %all-reduce.80.cloned.1.call-done = (f32[192,256]{1,0:T(8,128)}, f32[256,768]{1,0:T(8,128)}, f32[256,256]{1,0:T(8,128)}, f32[256,512]{1,0:T(8,128)}, f32[512,256]{1,0:T(8,128)}, /*index=5*/f32[256,192]{0,1:T(8,128)}) async-done(((f32[192,256]{1,0:T(8,128)}, f32[256,768]{1,0:T(8,128)}, f32[256,256]{1,0:T(8,128)}, f32[256,512]{1,0:T(8,128)}, f32[512,256]{1,0:T(8,128)}, /*index=5*/f32[256,192]{0,1:T(8,128)}), ...) | async-done | bytes 2490384 | tf_op jit(solution)/shard_map/psum | solution.py:162
  545.5 2.9 collective-permute-start.13
  548.4 2.4 collective-permute-start.12
  550.9 51.0 %all-reduce.73 = (f32[256]{0:T(256)S(1)}, f32[256]{0:T(256)S(1)}) all-reduce(f32[256]{0:T(256)S(1)} %add.401, f32[256]{0:T(256)S(1)} %add.404), channel_id=1, replica_groups=mesh['gx'=32,'gy'=16] {'gx'}, use_global_device_ids=true, to_apply=%region_20.21 | all-reduce | flops 512 | bytes 4096 | tf_op jit(solution)/shard_map/psum | solution.py:162
  601.9 67.6 %all-reduce.75 = (f32[256]{0:T(256)S(1)}, f32[256]{0:T(256)S(1)}) all-reduce(f32[256]{0:T(256)S(1)} %get-tuple-element.20, f32[256]{0:T(256)S(1)} %get-tuple-element.21), channel_id=1, replica_groups=mesh['gx'=32,'gy'=16] {'gy'}, use_global_device_ids=true, to_apply=%region_21.22 | all-reduce | flops 512 | bytes 4096 | tf_op jit(solution)/shard_map/psum | solution.py:162
  670.1 2.5 collective-permute-start.15
  672.7 4.5 collective-permute-start.14
  677.8 2.4 collective-permute-done.15
  681.1 50.3 %all-reduce.82.cloned.1.call-done = (f32[192,256]{1,0:T(8,128)}, f32[256,768]{1,0:T(8,128)}, f32[256,256]{1,0:T(8,128)}, f32[256,512]{1,0:T(8,128)}, f32[512,256]{1,0:T(8,128)}, /*index=5*/f32[256,192]{0,1:T(8,128)}) async-done(((f32[192,256]{1,0:T(8,128)}, f32[256,768]{1,0:T(8,128)}, f32[256,256]{1,0:T(8,128)}, f32[256,512]{1,0:T(8,128)}, f32[512,256]{1,0:T(8,128)}, /*index=5*/f32[256,192]{0,1:T(8,128)}), ...) | async-done | bytes 2490384 | tf_op jit(solution)/shard_map/psum | solution.py:162
  733.1 2.1 broadcast_multiply_fusion
  (597 shorter events, 125.5 us)
Async XLA Ops:
  7.2 45.8 %copy-start = (f32[256,768]{1,0:T(8,128)S(1)}, f32[256,768]{1,0:T(8,128)}, u32[]{:S(2)}) copy-start(f32[256,768]{1,0:T(8,128)} %param.14) | copy-start | bytes 2359300
  7.2 537.2 %all-reduce.80.cloned.1.call-start = ((), (), s32[]{:S(2)}) async-start(), calls=%async_computation | async-start | bytes 4980736 | tf_op jit(solution)/shard_map/psum | solution.py:162
  8.1 17.9 %collective-permute-start.1 = (f32[4,8,192]{2,1,0:T(8,128)S(1)}, f32[4,8,192]{2,1,0:T(8,128)S(1)}, u32[]{:S(2)}, u32[]{:S(2)}) collective-permute-start(f32[4,8,192]{2,1,0:T(8,128)S(1)} %get-tuple-element.163), channel_id=1, source_target_pairs={{0,16},{16,32},{32,48},{48,64},{64,80},{80,96},{96,112},{112,128},... | collective-permute-start | bytes 73736 | tf_op jit(solution)/shard_map/ppermute | solution.py:22
  12.0 14.9 %collective-permute-start = (f32[4,8,192]{2,1,0:T(8,128)S(1)}, f32[4,8,192]{2,1,0:T(8,128)S(1)}, u32[]{:S(2)}, u32[]{:S(2)}) collective-permute-start(f32[4,8,192]{2,1,0:T(8,128)S(1)} %get-tuple-element.162), channel_id=1, source_target_pairs={{16,0},{32,16},{48,32},{64,48},{80,64},{96,80},{112,96},{128,112},... | collective-permute-start | bytes 73736 | tf_op jit(solution)/shard_map/ppermute | solution.py:23
  26.9 10.4 %copy-start.36 = (f32[16,8,192]{2,1,0:T(8,128)}, f32[16,8,192]{2,1,0:T(8,128)S(1)}, u32[]{:S(2)}) copy-start(f32[16,8,192]{2,1,0:T(8,128)S(1)} %constant_dynamic-update-slice_fusion) | copy-start | bytes 294916
  27.5 7.8 %collective-permute-start.2 = (f32[16,4,192]{2,1,0:T(4,128)S(1)}, f32[16,4,192]{2,1,0:T(4,128)S(1)}, u32[]{:S(2)}, u32[]{:S(2)}) collective-permute-start(f32[16,4,192]{2,1,0:T(4,128)S(1)} %get-tuple-element.131), channel_id=1, source_target_pairs={{1,0},{2,1},{3,2},{4,3},{5,4},{6,5},{7,6},{8,7},{9,8},{10,9},{11,1... | collective-permute-start | bytes 147464 | tf_op jit(solution)/shard_map/ppermute | solution.py:23
  30.4 7.0 collective-permute-start.3
  34.6 33.2 %copy-start.191 = (pred[192]{0:T(512)(128)(4,1)}, pred[192]{0:T(512)(128)(4,1)S(1)}, u32[]{:S(2)}) copy-start(pred[192]{0:T(512)(128)(4,1)S(1)} %get-tuple-element.185) | copy-start | bytes 580
  34.6 33.2 %copy-start.196 = (pred[192]{0:T(512)(128)(4,1)}, pred[192]{0:T(512)(128)(4,1)S(1)}, u32[]{:S(2)}) copy-start(pred[192]{0:T(512)(128)(4,1)S(1)} %get-tuple-element.184) | copy-start | bytes 580
  43.1 6.6 copy-start.33
  69.2 6.0 collective-permute-start.4
  72.0 6.8 collective-permute-start.5
  75.2 21.8 %copy-start.103 = (f32[4,8,192]{2,1,0:T(8,128)}, f32[4,8,192]{2,1,0:T(8,128)S(1)}, u32[]{:S(2)}) copy-start(f32[4,8,192]{2,1,0:T(8,128)S(1)} %collective-permute-done.4) | copy-start | bytes 73732
  78.7 18.3 %copy-start.104 = (f32[4,8,192]{2,1,0:T(8,128)}, f32[4,8,192]{2,1,0:T(8,128)S(1)}, u32[]{:S(2)}) copy-start(f32[4,8,192]{2,1,0:T(8,128)S(1)} %collective-permute-done.5) | copy-start | bytes 73732
  78.8 12.5 %collective-permute-start.6 = (f32[16,4,192]{2,1,0:T(4,128)S(1)}, f32[16,4,192]{2,1,0:T(4,128)S(1)}, u32[]{:S(2)}, u32[]{:S(2)}) collective-permute-start(f32[16,4,192]{2,1,0:T(4,128)S(1)} %get-tuple-element.129), channel_id=1, source_target_pairs={{1,0},{2,1},{3,2},{4,3},{5,4},{6,5},{7,6},{8,7},{9,8},{10,9},{11,1... | collective-permute-start | bytes 147464 | tf_op jit(solution)/shard_map/ppermute | solution.py:23
  88.7 3.2 collective-permute-start.7
  91.3 5.8 copy-start.98
  135.3 5.6 copy-start.21
  135.3 6.1 copy-start.17
  159.9 9.3 %copy-start.44 = (f32[2,2,16,256]{2,3,1,0:T(8,128)S(1)}, f32[2,2,16,256]{2,3,1,0:T(8,128)}, u32[]{:S(2)}) copy-start(f32[2,2,16,256]{2,3,1,0:T(8,128)} %get-tuple-element.74) | copy-start | bytes 196612
  161.8 8.2 %copy-start.43 = (f32[2,2,16,256]{2,3,1,0:T(8,128)S(1)}, f32[2,2,16,256]{2,3,1,0:T(8,128)}, u32[]{:S(2)}) copy-start(f32[2,2,16,256]{2,3,1,0:T(8,128)} %get-tuple-element.67) | copy-start | bytes 196612
  173.7 9.3 %copy-start.48 = (f32[2,2,16,256]{2,3,1,0:T(8,128)S(1)}, f32[2,2,16,256]{2,3,1,0:T(8,128)}, u32[]{:S(2)}) copy-start(f32[2,2,16,256]{2,3,1,0:T(8,128)} %get-tuple-element.63) | copy-start | bytes 196612
  175.5 8.2 %copy-start.46 = (f32[2,2,16,256]{2,3,1,0:T(8,128)S(1)}, f32[2,2,16,256]{2,3,1,0:T(8,128)}, u32[]{:S(2)}) copy-start(f32[2,2,16,256]{2,3,1,0:T(8,128)} %get-tuple-element.64) | copy-start | bytes 196612
  203.1 21.2 %copy-start.156 = (f32[2,2,8,16]{3,2,1,0:T(8,128)S(1)}, f32[2,2,8,16]{3,2,1,0:T(8,128)}, u32[]{:S(2)}) copy-start(f32[2,2,8,16]{3,2,1,0:T(8,128)} %copy-done.155) | copy-start | bytes 6148
  203.3 22.5 %copy-start.194 = (pred[8]{0:T(512)(128)(4,1)S(1)}, pred[8]{0:T(512)(128)(4,1)}, u32[]{:S(2)}) copy-start(pred[8]{0:T(512)(128)(4,1)} %constant.73.clone.1) | copy-start | bytes 28
  203.5 22.4 %copy-start.102 = (f32[8,8,64]{2,1,0:T(8,128)S(1)}, f32[8,8,64]{2,1,0:T(8,128)}, u32[]{:S(2)}) copy-start(f32[8,8,64]{2,1,0:T(8,128)} %get-tuple-element.160) | copy-start | bytes 49156
  203.6 5.5 collective-permute-start.9
  205.5 21.2 %copy-start.37 = (f32[16,8,192]{2,1,0:T(8,128)S(1)}, f32[16,8,192]{2,1,0:T(8,128)}, u32[]{:S(2)}) copy-start(f32[16,8,192]{2,1,0:T(8,128)} %copy-done.36) | copy-start | bytes 294916
  205.5 21.1 %copy-start.86 = (f32[8,8,191]{2,1,0:T(8,128)S(1)}, f32[8,8,191]{2,1,0:T(8,128)}, u32[]{:S(2)}) copy-start(f32[8,8,191]{2,1,0:T(8,128)} %get-tuple-element.157) | copy-start | bytes 146692
  205.5 21.1 %copy-start.87 = (f32[8,8,191]{2,1,0:T(8,128)S(1)}, f32[8,8,191]{2,1,0:T(8,128)}, u32[]{:S(2)}) copy-start(f32[8,8,191]{2,1,0:T(8,128)} %get-tuple-element.158) | copy-start | bytes 146692
  205.5 21.1 %copy-start.89 = (f32[16,4,192]{2,1,0:T(4,128)S(1)}, f32[16,4,192]{2,1,0:T(4,128)}, u32[]{:S(2)}) copy-start(f32[16,4,192]{2,1,0:T(4,128)} %copy-done.88) | copy-start | bytes 147460
  205.5 21.1 %copy-start.91 = (f32[16,4,192]{2,1,0:T(4,128)S(1)}, f32[16,4,192]{2,1,0:T(4,128)}, u32[]{:S(2)}) copy-start(f32[16,4,192]{2,1,0:T(4,128)} %copy-done.90) | copy-start | bytes 147460
  205.5 21.1 %copy-start.116 = (f32[4,8,192]{2,1,0:T(8,128)S(1)}, f32[4,8,192]{2,1,0:T(8,128)}, u32[]{:S(2)}) copy-start(f32[4,8,192]{2,1,0:T(8,128)} %copy-done.115) | copy-start | bytes 73732
  205.5 21.1 %copy-start.118 = (f32[4,8,192]{2,1,0:T(8,128)S(1)}, f32[4,8,192]{2,1,0:T(8,128)}, u32[]{:S(2)}) copy-start(f32[4,8,192]{2,1,0:T(8,128)} %copy-done.117) | copy-start | bytes 73732
  205.6 21.1 %copy-start.120 = (f32[8,8,64]{2,1,0:T(8,128)S(1)}, f32[8,8,64]{2,1,0:T(8,128)}, u32[]{:S(2)}) copy-start(f32[8,8,64]{2,1,0:T(8,128)} %get-tuple-element.161) | copy-start | bytes 49156
  205.6 21.1 %copy-start.197 = (pred[192]{0:T(512)(128)(4,1)S(1)}, pred[192]{0:T(512)(128)(4,1)}, u32[]{:S(2)}) copy-start(pred[192]{0:T(512)(128)(4,1)} %copy-done.196) | copy-start | bytes 580
  205.6 7.3 collective-permute-start.8
  212.9 12.0 %collective-permute-start.11 = (f32[24,4,192]{2,1,0:T(4,128)S(1)}, f32[24,4,192]{2,1,0:T(4,128)S(1)}, u32[]{:S(2)}, u32[]{:S(2)}) collective-permute-start(f32[24,4,192]{2,1,0:T(4,128)S(1)} %get-tuple-element.117), channel_id=1, source_target_pairs={{1,0},{2,1},{3,2},{4,3},{5,4},{6,5},{7,6},{8,7},{9,8},{10,9},{11,1... | collective-permute-start | bytes 221192 | tf_op jit(solution)/shard_map/ppermute | solution.py:23
  222.1 3.5 collective-permute-start.10
  230.4 5.6 copy-start.185
  230.4 6.3 copy-start.22
  230.4 6.8 copy-start.14
  248.6 9.3 %copy-start.47 = (f32[2,2,16,256]{2,3,1,0:T(8,128)S(1)}, f32[2,2,16,256]{2,3,1,0:T(8,128)}, u32[]{:S(2)}) copy-start(f32[2,2,16,256]{2,3,1,0:T(8,128)} %get-tuple-element.55) | copy-start | bytes 196612
  250.5 8.2 %copy-start.45 = (f32[2,2,16,256]{2,3,1,0:T(8,128)S(1)}, f32[2,2,16,256]{2,3,1,0:T(8,128)}, u32[]{:S(2)}) copy-start(f32[2,2,16,256]{2,3,1,0:T(8,128)} %get-tuple-element.56) | copy-start | bytes 196612
  262.9 7.4 copy-start.50
  262.9 8.3 %copy-start.49 = (f32[2,2,16,256]{2,3,1,0:T(8,128)S(1)}, f32[2,2,16,256]{2,3,1,0:T(8,128)}, u32[]{:S(2)}) copy-start(f32[2,2,16,256]{2,3,1,0:T(8,128)} %get-tuple-element.45) | copy-start | bytes 196612
  291.6 107.7 %copy-start.35 = (f32[192,256]{1,0:T(8,128)S(1)}, f32[192,256]{1,0:T(8,128)}, u32[]{:S(2)}) copy-start(f32[192,256]{1,0:T(8,128)} %param.12) | copy-start | bytes 589828
  291.6 107.7 %copy-start.175 = (f32[256]{0:T(256)S(1)}, f32[256]{0:T(256)}, u32[]{:S(2)}) copy-start(f32[256]{0:T(256)} %param.13) | copy-start | bytes 3076
  292.9 438.4 %all-reduce.82.cloned.1.call-start = ((), (), s32[]{:S(2)}) async-start(), calls=%async_computation.1 | async-start | bytes 4980736 | tf_op jit(solution)/shard_map/psum | solution.py:162
  412.0 132.5 %copy-start.110 = (f32[8,8,192]{2,1,0:T(8,128)S(1)}, f32[8,8,192]{2,1,0:T(8,128)}, u32[]{:S(2)}) copy-start(f32[8,8,192]{2,1,0:T(8,128)} %get-tuple-element.138) | copy-start | bytes 147460
  412.0 132.5 %copy-start.109 = (f32[8,8,192]{2,1,0:T(8,128)S(1)}, f32[8,8,192]{2,1,0:T(8,128)}, u32[]{:S(2)}) copy-start(f32[8,8,192]{2,1,0:T(8,128)} %get-tuple-element.139) | copy-start | bytes 147460
  412.0 132.6 %copy-start.82 = (f32[8,8,192]{2,1,0:T(8,128)S(1)}, f32[8,8,192]{2,1,0:T(8,128)}, u32[]{:S(2)}) copy-start(f32[8,8,192]{2,1,0:T(8,128)} %get-tuple-element.140) | copy-start | bytes 147460
  412.0 132.6 %copy-start.83 = (f32[8,8,192]{2,1,0:T(8,128)S(1)}, f32[8,8,192]{2,1,0:T(8,128)}, u32[]{:S(2)}) copy-start(f32[8,8,192]{2,1,0:T(8,128)} %get-tuple-element.142) | copy-start | bytes 147460
  412.1 132.6 %copy-start.193 = (pred[192]{0:T(512)(128)(4,1)S(1)}, pred[192]{0:T(512)(128)(4,1)}, u32[]{:S(2)}) copy-start(pred[192]{0:T(512)(128)(4,1)} %copy-done.191) | copy-start | bytes 580
  412.1 132.6 %copy-start.203 = (pred[191]{0:T(512)(128)(4,1)S(1)}, pred[191]{0:T(512)(128)(4,1)}, u32[]{:S(2)}) copy-start(pred[191]{0:T(512)(128)(4,1)} %slice.447) | copy-start | bytes 577
  544.4 6.4 copy-start.199
  544.4 6.4 copy-start.201
  544.5 6.4 copy-start.198
  544.5 6.4 copy-start.200
  545.4 134.9 %copy-start.195 = (pred[8]{0:T(512)(128)(4,1)S(1)}, pred[8]{0:T(512)(128)(4,1)}, u32[]{:S(2)}) copy-start(pred[8]{0:T(512)(128)(4,1)} %constant.73.clone.1) | copy-start | bytes 28
  545.5 124.6 %collective-permute-start.13 = (f32[4,16,192]{2,1,0:T(8,128)S(1)}, f32[4,16,192]{2,1,0:T(8,128)S(1)}, u32[]{:S(2)}, u32[]{:S(2)}) collective-permute-start(f32[4,16,192]{2,1,0:T(8,128)S(1)} %get-tuple-element.119), channel_id=1, source_target_pairs={{16,0},{32,16},{48,32},{64,48},{80,64},{96,80},{112,96},{128,112},... | collective-permute-start | bytes 147464 | tf_op jit(solution)/shard_map/ppermute | solution.py:23
  548.4 121.7 %collective-permute-start.12 = (f32[4,16,192]{2,1,0:T(8,128)S(1)}, f32[4,16,192]{2,1,0:T(8,128)S(1)}, u32[]{:S(2)}, u32[]{:S(2)}) collective-permute-start(f32[4,16,192]{2,1,0:T(8,128)S(1)} %get-tuple-element.118), channel_id=1, source_target_pairs={{0,16},{16,32},{32,48},{48,64},{64,80},{80,96},{96,112},{112,128},... | collective-permute-start | bytes 147464 | tf_op jit(solution)/shard_map/ppermute | solution.py:22
  670.1 10.0 %collective-permute-start.15 = (f32[24,4,192]{2,1,0:T(4,128)S(1)}, f32[24,4,192]{2,1,0:T(4,128)S(1)}, u32[]{:S(2)}, u32[]{:S(2)}) collective-permute-start(f32[24,4,192]{2,1,0:T(4,128)S(1)} %get-tuple-element.115), channel_id=1, source_target_pairs={{1,0},{2,1},{3,2},{4,3},{5,4},{6,5},{7,6},{8,7},{9,8},{10,9},{11,1... | collective-permute-start | bytes 221192 | tf_op jit(solution)/shard_map/ppermute | solution.py:23
  672.7 7.5 %collective-permute-start.14 = (f32[24,4,192]{2,1,0:T(4,128)S(1)}, f32[24,4,192]{2,1,0:T(4,128)S(1)}, u32[]{:S(2)}, u32[]{:S(2)}) collective-permute-start(f32[24,4,192]{2,1,0:T(4,128)S(1)} %get-tuple-element.114), channel_id=1, source_target_pairs={{0,1},{1,2},{2,3},{3,4},{4,5},{5,6},{6,7},{7,8},{8,9},{9,10},{10,1... | collective-permute-start | bytes 221192 | tf_op jit(solution)/shard_map/ppermute | solution.py:22
  (158 other events, 436.0 us)
Sparse Core Ops, SparseCore 0:
  293.1 251.2 all-reduce.79
  547.8 183.5 all-reduce.81
